TPU v7x, 32 devices: a whole 2x2x4 slice. The times are simulated.
32 devices in a mesh: row: 8 (over z, y), col: 4 (over x, core).
Axes of the slice: x: 2, y: 2, z: 4, core: 2. Of those that a mesh axis runs over, the one named last changes fastest.
Arguments:
- valence: bfloat16 [32768, 2048], P('row', 'col')
- conduction: bfloat16 [32768, 1024], P('row', 'col')
- point_index: int32 [8192], replicated, may hold values from 0 to 32767, as said below
Outputs:
- gram: float32 [8192, 8192], P('col', 'row')
Inputs may be any that keep to these rules, and one draw needn't show every extreme that they name: `point_index`: 8192 distinct cells; cell g lies in slab g // 4096. In each aligned block of 1024 entries, at most 256 lie in any one slab, and in every block some slab holds exactly 256.
All inputs are finite; a program needn't handle non-finite values.
Results may differ from a plain program's by a relative error of at most 0.0003.
Values may be sent and summed in bfloat16 or wider, within the bound.
A program may use at most 128 MiB of HBM per device.

v0:
```python
import functools

import jax
import jax.numpy as jnp
from jax import lax
from jax.experimental import pallas as pl
from jax.experimental.pallas import tpu as pltpu
from jax.sharding import PartitionSpec as P

MESH = pl.DeviceIdType.MESH
CHUNK_ROWS = 16
GROUP = 8
COLUMN_TILE = 256


def spread_kernel(
    n, c, wv, w, half,
    x_ref, o_ref, own, full, own_sem, peer_send, peer_recv, mate_send, mate_recv, ring_send, ring_recv,
):
    span = n // c
    pairs = c // 2
    chunks = half // CHUNK_ROWS
    stage_rows = half // GROUP
    group_rows = GROUP * CHUNK_ROWS
    stride = GROUP // (2 * half // COLUMN_TILE)
    row, col = lax.axis_index("row"), lax.axis_index("col")
    core, chip = lax.rem(col, 2), col // 2
    mate = chip * 2 + 1 - core

    def position(r):
        y, z = lax.rem(r, 2), r // 2
        return (1 - y) * z + y * (n - 1 - z)

    def row_at(p):
        back = p // (n // 2)
        return (1 - back) * (2 * p) + back * (2 * (n - 1 - p) + 1)

    here = position(row)
    right, left = row_at(lax.rem(here + 1, n)), row_at(lax.rem(here + n - 1, n))

    barrier = pltpu.get_barrier_semaphore()
    for other in (left, right):
        pl.semaphore_signal(barrier, inc=1, device_id=(other, col), device_id_type=MESH)
    for q in range(1, c):
        pl.semaphore_signal(
            barrier, inc=1, device_id=(row, lax.rem(col + q, c)), device_id_type=MESH
        )

    def piece(owner, first, count):
        return own.at[pl.ds(first, count), pl.ds(pl.multiple_of(owner * w, 128), w)]

    mine = pltpu.make_async_copy(x_ref, piece(col, 0, 2 * half), own_sem)
    mine.start()
    pl.semaphore_wait(barrier, 2 + c - 1)
    mine.wait()

    def stage_first(m, h):
        return pl.multiple_of(h * half + m * stage_rows, stage_rows)

    def to_peer(q, owner, m, h):
        ref = piece(owner, stage_first(m, h), stage_rows)
        return pltpu.make_async_remote_copy(
            src_ref=ref, dst_ref=ref,
            send_sem=peer_send.at[q - 1], recv_sem=peer_recv.at[q - 1, m, h],
            device_id=(row, lax.rem(chip + q, pairs) * 2 + core), device_id_type=MESH,
        )

    def to_mate(q, owner, m, h):
        ref = piece(owner, stage_first(m, h), stage_rows)
        return pltpu.make_async_remote_copy(
            src_ref=ref, dst_ref=ref,
            send_sem=mate_send.at[q], recv_sem=mate_recv.at[q, m, h],
            device_id=(row, mate), device_id_type=MESH,
        )

    def send_own(m, _):
        for h in range(2):
            for q in range(1, pairs):
                to_peer(q, col, m, h).start()
            to_mate(0, col, m, h).start()
        return 0

    lax.fori_loop(0, GROUP, send_own, 0)

    def stream(i, t):
        s, back = i // 2, lax.rem(i, 2)
        source = position(span * col + s)
        distance = lax.rem((1 - back) * (here - source) + back * (source - here) + n, n)
        return s, back, distance, t - distance

    def ring_copy(i, k, s, back, source_ref, source_first):
        first = pl.multiple_of(s * 2 * half + back * half + k * CHUNK_ROWS, CHUNK_ROWS)
        return pltpu.make_async_remote_copy(
            src_ref=source_ref.at[pl.ds(pl.multiple_of(source_first, CHUNK_ROWS), CHUNK_ROWS)],
            dst_ref=full.at[pl.ds(first, CHUNK_ROWS)],
            send_sem=ring_send.at[i], recv_sem=ring_recv.at[i, k],
            device_id=((1 - back) * right + back * left, col), device_id_type=MESH,
        )

    def step(t, _):
        @pl.when(t < GROUP)
        def _():
            for h in range(2):
                for q in range(1, pairs):
                    owner = lax.rem(chip - q + pairs, pairs) * 2 + core
                    to_peer(q, owner, t, h).wait_recv()
                    to_mate(q, owner, t, h).start()
            for h in range(2):
                for q in range(pairs):
                    owner = lax.rem(chip - q + pairs, pairs) * 2 + 1 - core
                    to_mate(q, owner, t, h).wait_recv()

        def forward(i, _):
            s, back, distance, k = stream(i, t)

            @pl.when((k >= 0) & (k < chunks))
            def _():
                in_block = back * half + k * CHUNK_ROWS

                @pl.when(distance == 0)
                def _():
                    ring_copy(i, k, s, back, own, in_block).start()

                @pl.when(distance > 0)
                def _():
                    copy = ring_copy(i, k, s, back, full, s * 2 * half + in_block)
                    copy.wait_recv()

                    @pl.when(distance < n - 1)
                    def _():
                        copy.start()

            return 0

        lax.fori_loop(0, 2 * span, forward, 0)

        def compute(i, _):
            s, back, distance, k = stream(i, t)
            since = k - (GROUP - 1)
            phase = lax.rem(since + GROUP, GROUP)

            @pl.when((since >= 0) & (since < chunks) & (lax.rem(phase, stride) == 0))
            def _():
                in_block = pl.multiple_of(back * half + (since - phase) * CHUNK_ROWS, group_rows)
                first = pl.multiple_of(s * 2 * half + in_block, group_rows)
                begin = pl.multiple_of(phase // stride * COLUMN_TILE, COLUMN_TILE)

                @pl.when((distance == 0) & (phase == 0))
                def _():
                    full[pl.ds(first, group_rows), :] = own[pl.ds(in_block, group_rows), :]

                totals = []
                for low, high in ((0, wv), (wv, w)):
                    total = None
                    for p in range(c):
                        part = lax.dot_general(
                            full[pl.ds(first, group_rows), p * w + low : p * w + high],
                            own[pl.ds(begin, COLUMN_TILE), p * w + low : p * w + high],
                            (((1,), (1,)), ((), ())),
                            preferred_element_type=jnp.float32,
                        )
                        total = part if total is None else total + part
                    totals.append(total)
                o_ref[pl.ds(first, group_rows), pl.ds(begin, COLUMN_TILE)] = totals[0] * totals[1]

            return 0

        lax.fori_loop(0, 2 * span, compute, 0)
        return 0

    lax.fori_loop(0, chunks + n - 1 + GROUP - 1, step, 0)

    whole = piece(col, 0, 2 * half)
    for q in range(pairs):
        if q >= 1:
            pltpu.make_async_copy(whole, whole, peer_send.at[q - 1]).wait()
        pltpu.make_async_copy(whole, whole, mate_send.at[q]).wait()

    def drain(i, _):
        distance = stream(i, 0)[2]

        @pl.when(distance < n - 1)
        def _():
            stretch = full.at[pl.ds(0, half)]
            pltpu.make_async_copy(stretch, stretch, ring_send.at[i]).wait()

        return 0

    lax.fori_loop(0, 2 * span, drain, 0)


def spread_and_multiply(x, wv, n, c):
    points, w = x.shape
    span = n // c
    half = points // 2
    chunks = half // CHUNK_ROWS
    pairs = c // 2
    return pl.pallas_call(
        functools.partial(spread_kernel, n, c, wv, w, half),
        out_shape=pltpu.VMEM((span * points, points), jnp.float32),
        in_specs=[pl.BlockSpec(memory_space=pl.ANY)],
        out_specs=pl.BlockSpec(memory_space=pltpu.VMEM),
        scratch_shapes=[
            pltpu.VMEM((points, c * w), jnp.bfloat16),
            pltpu.VMEM((span * points, c * w), jnp.bfloat16),
            pltpu.SemaphoreType.DMA,
            pltpu.SemaphoreType.DMA((max(pairs - 1, 1),)),
            pltpu.SemaphoreType.DMA((max(pairs - 1, 1), GROUP, 2)),
            pltpu.SemaphoreType.DMA((pairs,)),
            pltpu.SemaphoreType.DMA((pairs, GROUP, 2)),
            pltpu.SemaphoreType.DMA((2 * span,)),
            pltpu.SemaphoreType.DMA((2 * span, chunks)),
        ],
        compiler_params=pltpu.CompilerParams(
            collective_id=0, has_side_effects=True, vmem_limit_bytes=32 * 1024 * 1024
        ),
    )(x)


def on_device(valence, conduction, point_index):
    row_count = lax.axis_size("row")
    col_count = lax.axis_size("col")
    my_row = lax.axis_index("row")
    grid_cells = valence.shape[0]
    total_points = point_index.shape[0]
    block_points = total_points // row_count
    capacity = max(2 * block_points // row_count, 2)
    blocks = point_index.reshape(row_count, block_points)
    owners = blocks // grid_cells
    offsets = blocks - owners * grid_cells
    onehot = owners[:, None, :] == jnp.arange(row_count, dtype=jnp.int32)[None, :, None]
    place = jnp.arange(block_points, dtype=jnp.int32)
    earlier = (place[:, None] < place[None, :]).astype(jnp.bfloat16)
    before = lax.dot_general(
        onehot.astype(jnp.bfloat16), earlier, (((2,), (0,)), ((), ())),
        preferred_element_type=jnp.float32,
    )
    ranks = jnp.sum(jnp.where(onehot, before, 0.0), axis=1).astype(jnp.int32)
    owned = owners == my_row
    picked = owned[:, None, :] & (
        ranks[:, None, :] == jnp.arange(capacity, dtype=jnp.int32)[None, :, None]
    )
    source_cells = jnp.sum(jnp.where(picked, offsets[:, None, :], 0), axis=2)
    own_owner = lax.dynamic_index_in_dim(owners, my_row, 0, keepdims=False)
    own_rank = lax.dynamic_index_in_dim(ranks, my_row, 0, keepdims=False)
    flat_slot = own_owner * capacity + own_rank

    def route(array):
        send = array.at[source_cells].get(mode="promise_in_bounds")
        got = lax.all_to_all(send, "row", split_axis=0, concat_axis=0, tiled=True)
        got = got.reshape(row_count * capacity, got.shape[2])
        return got.at[flat_slot].get(mode="promise_in_bounds")

    rows = jnp.concatenate([route(valence), route(conduction)], axis=1)
    return spread_and_multiply(rows, valence.shape[1], row_count, col_count)


def solution(mesh):
    placed = (P("row", "col"), P("row", "col"), P())
    return jax.shard_map(
        on_device, mesh=mesh, in_specs=placed, out_specs=P("col", "row"), check_vma=False
    )
```

profile of v0, /device:TPU:0, one launch (start us, length us, event | category | flops | bytes accessed | tf_op | source)
XLA Modules:
  0.0 288.2 jit_solution(3225002251953019800)
XLA Ops:
  0.0 0.0 copy-start
  0.0 0.9 reshape.109
  1.0 0.4 fusion.7
  1.4 1.8 select_reduce_fusion
  3.3 0.0 copy-done
  3.3 9.0 %gather_fusion.2 = bf16[2048,256]{1,0:T(8,128)(2,1)} fusion(bf16[4096,256]{1,0:T(8,128)(2,1)S(1)} %copy-done, s32[2048]{0:T(1024)S(1)} %broadcast_clamp_fusion), kind=kCustom, calls=%fused_computation.2 | custom fusion | bytes 2105344 | tf_op jit(solution)/shard_map/gather | solution.py:249
  12.3 7.3 %all-to-all-start.1 = ((bf16[8,256,256]{2,1,0:T(8,128)(2,1)}), bf16[8,256,256]{2,1,0:T(8,128)(2,1)S(1)}, u32[]{:S(2)}, u32[]{:S(2)}) async-start(bf16[8,256,256]{2,1,0:T(8,128)(2,1)} %bitcast.22), calls=%async_computation.1 | async-start | bytes 2097152 | tf_op jit(solution)/shard_map/all_to_all | solution.py:250
  19.6 12.0 %gather_fusion = bf16[2048,512]{1,0:T(8,128)(2,1)} fusion(bf16[4096,512]{1,0:T(8,128)(2,1)} %param.3, s32[2048]{0:T(1024)S(1)} %broadcast_clamp_fusion), kind=kCustom, calls=%fused_computation | custom fusion | bytes 4202496 | tf_op jit(solution)/shard_map/gather | solution.py:249
  31.6 13.8 %all-to-all-done.1 = bf16[8,256,256]{2,1,0:T(8,128)(2,1)S(1)} async-done(((bf16[8,256,256]{2,1,0:T(8,128)(2,1)}), bf16[8,256,256]{2,1,0:T(8,128)(2,1)S(1)}, u32[]{:S(2)}, u32[]{:S(2)}) %all-to-all-start.1) | async-done | bytes 1048608 | tf_op jit(solution)/shard_map/all_to_all | solution.py:250
  45.4 4.3 %all-to-all-start = ((bf16[8,256,512]{2,1,0:T(8,128)(2,1)}), bf16[8,256,512]{2,1,0:T(8,128)(2,1)}, u32[]{:S(2)}, u32[]{:S(2)}) async-start(bf16[8,256,512]{2,1,0:T(8,128)(2,1)} %bitcast.21), calls=%async_computation | async-start | bytes 4194304 | tf_op jit(solution)/shard_map/all_to_all | solution.py:250
  49.8 5.0 %gather_fusion.3 = bf16[1024,256]{1,0:T(8,128)(2,1)} fusion(bf16[2048,256]{1,0:T(8,128)(2,1)S(1)} %bitcast.20, s32[1024]{0:T(1024)S(1)} %broadcast_clamp_fusion.1), kind=kCustom, calls=%fused_computation.3 | custom fusion | bytes 1052672 | tf_op jit(solution)/shard_map/gather | solution.py:252
  54.8 42.8 %all-to-all-done = bf16[8,256,512]{2,1,0:T(8,128)(2,1)} async-done(((bf16[8,256,512]{2,1,0:T(8,128)(2,1)}), bf16[8,256,512]{2,1,0:T(8,128)(2,1)}, u32[]{:S(2)}, u32[]{:S(2)}) %all-to-all-start) | async-done | bytes 2097184 | tf_op jit(solution)/shard_map/all_to_all | solution.py:250
  97.5 5.8 %gather_fusion.1 = bf16[1024,512]{1,0:T(8,128)(2,1)S(1)} fusion(bf16[2048,512]{1,0:T(8,128)(2,1)} %bitcast.3, s32[1024]{0:T(1024)S(1)} %broadcast_clamp_fusion.1), kind=kCustom, calls=%fused_computation.1 | custom fusion | bytes 2101248 | tf_op jit(solution)/shard_map/gather | solution.py:252
  103.4 1.1 pad_maximum_fusion.x_ref
  104.5 180.3 %shard_map.37 = f32[2048,1024]{1,0:T(8,128)S(1)} custom-call(bf16[1024,768]{1,0:T(8,128)(2,1)S(1)} %pad_maximum_fusion.x_ref), custom_call_target="tpu_custom_call" | custom-call | tf_op jit(solution)/shard_map/pallas_call | solution.py:198
  284.8 3.4 %copy.6 = f32[2048,1024]{1,0:T(8,128)} copy(f32[2048,1024]{1,0:T(8,128)S(1)} %shard_map.37) | data formatting | bytes 16777216
  (8 shorter events, 0.1 us)
Async XLA Ops:
  0.0 3.3 %copy-start = (bf16[4096,256]{1,0:T(8,128)(2,1)S(1)}, bf16[4096,256]{1,0:T(8,128)(2,1)}, u32[]{:S(2)}) copy-start(bf16[4096,256]{1,0:T(8,128)(2,1)} %param.4) | copy-start | bytes 6291460
  12.3 33.1 %all-to-all-start.1 = ((bf16[8,256,256]{2,1,0:T(8,128)(2,1)}), bf16[8,256,256]{2,1,0:T(8,128)(2,1)S(1)}, u32[]{:S(2)}, u32[]{:S(2)}) async-start(bf16[8,256,256]{2,1,0:T(8,128)(2,1)} %bitcast.22), calls=%async_computation.1 | async-start | bytes 2097152 | tf_op jit(solution)/shard_map/all_to_all | solution.py:250
  45.4 52.1 %all-to-all-start = ((bf16[8,256,512]{2,1,0:T(8,128)(2,1)}), bf16[8,256,512]{2,1,0:T(8,128)(2,1)}, u32[]{:S(2)}, u32[]{:S(2)}) async-start(bf16[8,256,512]{2,1,0:T(8,128)(2,1)} %bitcast.21), calls=%async_computation | async-start | bytes 4194304 | tf_op jit(solution)/shard_map/all_to_all | solution.py:250
where the time goes:
time: 290 us; the launch traced here: 288 us
  Pallas kernels  180 us (62%)
  waiting for transfers between devices  56.5 us (19%)
  local copies, waits for them, and re-layouts  36.2 us (12%)
  starting transfers between devices  11.7 us (4%)
  other arithmetic  3.07 us (1%)
    pallas_call x1, Pallas kernels, spread_and_multiply(): pl.pallas_call(functools.partial(spread_kernel, n, c, wv, w, half), out_s...  180 us
    all_to_all x2, waiting for transfers between devices, route(): got = lax.all_to_all(send, 'row', split_axis=0, concat_axis=0, tiled=True)  56.5 us
    gather x2, local copies, waits for them, and re-layouts, route(): send = array.at[source_cells].get(mode='promise_in_bounds')  21 us
    all_to_all x2, starting transfers between devices, route(): got = lax.all_to_all(send, 'row', split_axis=0, concat_axis=0, tiled=True)  11.7 us
    gather x2, local copies, waits for them, and re-layouts, route(): return got.at[flat_slot].get(mode='promise_in_bounds')  10.8 us
  transfers between devices with their start and end apart: 2, of which 2 were waited for; matrix products, arithmetic and copies ran while one was open for 6% of the time, Pallas kernels for 0%

commit v1 on v0

v1 whole, which is shorter than its diff:
```python
import functools
import math

import jax
import jax.numpy as jnp
from jax import lax
from jax.experimental import pallas as pl
from jax.experimental.pallas import tpu as pltpu
from jax.sharding import PartitionSpec as P

MESH = pl.DeviceIdType.MESH
UNIT_ROWS = 256
TILE = 256
LEAD = 2


def gram_kernel(
    n, c, cap, kv, splits,
    xv_ref, xc_ref, slot_ref, o_ref,
    got, pick, full, own, cond,
    trade_send, trade_recv, up_send, down_send, pair_send, piece_recv, own_send, own_recv,
):
    chunks, _, g = got.shape
    points = slot_ref.shape[0]
    span = n // c
    pairs = c // 2
    m = n // 2
    rows_unit = points // splits
    units = chunks * splits
    share = n // splits
    row, col = lax.axis_index("row"), lax.axis_index("col")
    z, y = row // 2, lax.rem(row, 2)
    pair = row + 1 - 2 * y
    core, chip = lax.rem(col, 2), col // 2
    mate = chip * 2 + 1 - core
    home, home_s = row // span, lax.rem(row, span)
    home_core = lax.rem(home, 2)
    is_root = col == home
    is_peer = (core == home_core) & (col != home)
    is_far = core != home_core

    def part_of(j):
        t = lax.rem(j - 2 * col + 2 * n, n)
        return t // c, lax.rem(t, c)

    my_shard = part_of(row)[1]
    keeps = (my_shard == col).astype(jnp.int32)

    def trade_target(i):
        e = lax.rem(i + row, n)
        s, cd = e // c, lax.rem(e, c)
        return lax.rem(s * c + col + 2 * cd, n), cd, s

    barrier = pltpu.get_barrier_semaphore()

    def greet(r, k):
        pl.semaphore_signal(barrier, inc=1, device_id=(r, k), device_id_type=MESH)

    def greet_trade(i, _):
        target, cd, _ = trade_target(i)

        @pl.when((target != row) | (cd != col))
        def _():
            greet(target, cd)

        @pl.when((i != row) | (my_shard != col))
        def _():
            greet(i, my_shard)

        return 0

    lax.fori_loop(0, n, greet_trade, 0)

    @pl.when(z > 0)
    def _():
        greet(row - 2, col)

    @pl.when(z + 1 < m)
    def _():
        greet(row + 2, col)

    greet(pair, col)
    greet(row, mate)
    for p in range(1, pairs):
        greet(row, lax.rem(chip + p, pairs) * 2 + core)
    ends = (z > 0).astype(jnp.int32) + (z + 1 < m).astype(jnp.int32)
    pl.semaphore_wait(barrier, 2 * (n - keeps) + ends + 2 + pairs - 1)

    def trade(k, i):
        target, cd, s = trade_target(i)
        rows = pl.ds(pl.multiple_of((cd * span + s) * cap, cap), cap)
        dst = got.at[k, pl.ds(pl.multiple_of(row * cap, cap), cap)]

        def ship(src):
            stays = (target == row) & (cd == col)

            @pl.when(stays)
            def _():
                pltpu.make_async_copy(src, dst, trade_recv.at[k]).start()

            @pl.when(jnp.logical_not(stays))
            def _():
                pltpu.make_async_remote_copy(
                    src_ref=src, dst_ref=dst,
                    send_sem=trade_send.at[k], recv_sem=trade_recv.at[k],
                    device_id=(target, cd), device_id_type=MESH,
                ).start()

        @pl.when(k < kv)
        def _():
            ship(xv_ref.at[rows, pl.ds(pl.multiple_of(k * g, g), g)])

        @pl.when(k >= kv)
        def _():
            ship(xc_ref.at[rows, pl.ds(pl.multiple_of((k - kv) * g, g), g)])

    def trade_portion(p):
        k, first = p // splits, lax.rem(p, splits) * share

        def one(i, _):
            trade(k, first + i)
            return 0

        lax.fori_loop(0, share, one, 0)

    def opening(p, _):
        trade_portion(p)
        return 0

    lead = splits + min(LEAD, splits)
    lax.fori_loop(0, lead, opening, 0)

    lanes = 128

    def build_pick(a, _):
        first = pl.multiple_of(a * lanes, lanes)
        place = lax.broadcasted_iota(jnp.int32, (points, lanes), 1) + first
        chosen = slot_ref[...] == place
        pick[:, pl.ds(first, lanes)] = jnp.where(chosen, 1.0, 0.0).astype(jnp.bfloat16)
        return 0

    lax.fori_loop(0, n * cap // lanes, build_pick, 0)

    block = 128

    def clear(a, _):
        rows = pl.ds(pl.multiple_of(a * block, block), block)
        o_ref[rows, :] = jnp.zeros((block, points), jnp.float32)
        cond[rows, :] = jnp.zeros((block, points), jnp.float32)
        return 0

    lax.fori_loop(0, span * points // block, clear, 0)

    def unit_rows(u):
        return u // splits, pl.ds(pl.multiple_of(lax.rem(u, splits) * rows_unit, rows_unit), rows_unit)

    def unit(j, u):
        k, rows = unit_rows(u)
        return full.at[j, k, rows]

    def send(j, u, sems, target_row):
        ref = unit(j, u)
        return pltpu.make_async_remote_copy(
            src_ref=ref, dst_ref=ref,
            send_sem=sems.at[j], recv_sem=piece_recv.at[j, u],
            device_id=(target_row, col), device_id_type=MESH,
        )

    def own_copy(q, u, src, slot, target_col):
        k, rows = unit_rows(u)
        return pltpu.make_async_remote_copy(
            src_ref=src, dst_ref=own.at[q, k, rows],
            send_sem=own_send.at[slot], recv_sem=own_recv.at[q, u],
            device_id=(row, target_col), device_id_type=MESH,
        )

    def own_unit(q, u):
        k, rows = unit_rows(u)
        return own.at[q, k, rows]

    def go_up(j, u):
        @pl.when(z + 1 < m)
        def _():
            send(j, u, up_send, row + 2).start()

    def go_down(j, u):
        @pl.when(z > 0)
        def _():
            send(j, u, down_send, row - 2).start()

    def go_pair(j, u):
        send(j, u, pair_send, pair).start()

    def spread_own(j, u):
        s, q = part_of(j)

        @pl.when(is_root & (s == home_s))
        def _():
            for p in range(1, pairs):
                own_copy(q, u, unit(j, u), p, lax.rem(chip + p, pairs) * 2 + core).start()
            own_copy(q, u, unit(j, u), 0, mate).start()

    def arrived(j, u):
        send(j, u, pair_send, pair).wait_recv()

    def compact(v):
        k, rows = unit_rows(v)

        @pl.when(lax.rem(v, splits) == 0)
        def _():
            pltpu.make_async_copy(got.at[k], got.at[k], trade_recv.at[k]).wait()

        dense = lax.dot_general(
            pick[rows, :], got[k], (((1,), (0,)), ((), ())), preferred_element_type=jnp.float32
        )
        full[row, k, rows, :] = dense.astype(jnp.bfloat16)

    def multiply(k, i):
        s, q = i // c, lax.rem(i, c)
        j = lax.rem(i + 2 * col, n)
        rows = pl.ds(pl.multiple_of(s * points, points), points)

        def tile(a, _):
            cols = pl.ds(pl.multiple_of(a * min(TILE, points), min(TILE, points)), min(TILE, points))
            part = lax.dot_general(
                full[j, k], own[q, k, cols, :], (((1,), (1,)), ((), ())),
                preferred_element_type=jnp.float32,
            )

            @pl.when(k < kv)
            def _():
                o_ref[rows, cols] += part

            @pl.when(k >= kv)
            def _():
                cond[rows, cols] += part

            return 0

        lax.fori_loop(0, points // min(TILE, points), tile, 0)

    compact(0)
    settle = m + 2 + splits - 1

    def step(t, _):
        @pl.when(t + lead < units)
        def _():
            trade_portion(t + lead)

        @pl.when(t < units)
        def _():
            go_up(row, t)
            go_down(row, t)
            go_pair(row, t)
            spread_own(row, t)

        def along(d, _):
            u = t - d

            @pl.when((u >= 0) & (u < units))
            def _():
                @pl.when(z >= d)
                def _():
                    j = row - 2 * d
                    arrived(j, u)
                    go_up(j, u)
                    go_pair(j, u)
                    spread_own(j, u)

                @pl.when(z + d < m)
                def _():
                    j = row + 2 * d
                    arrived(j, u)
                    go_down(j, u)
                    go_pair(j, u)
                    spread_own(j, u)

            return 0

        lax.fori_loop(1, m, along, 0)

        @pl.when(t + 1 < units)
        def _():
            compact(t + 1)

        def across(a, _):
            u = t - 1 - jnp.abs(a - z)

            @pl.when((u >= 0) & (u < units))
            def _():
                j = 2 * a + 1 - y
                arrived(j, u)
                spread_own(j, u)

            return 0

        lax.fori_loop(0, m, across, 0)

        def take_peer(q, _):
            u = t - m - 1

            @pl.when(is_peer & (u >= 0) & (u < units))
            def _():
                copy = own_copy(q, u, own_unit(q, u), 0, mate)
                copy.wait_recv()
                copy.start()

            return 0

        lax.fori_loop(0, c, take_peer, 0)

        def take_far(q, _):
            u = t - m - 2

            @pl.when(is_far & (u >= 0) & (u < units))
            def _():
                own_copy(q, u, own_unit(q, u), 0, mate).wait_recv()

            return 0

        lax.fori_loop(0, c, take_far, 0)

        w = t - settle

        @pl.when((w >= 0) & (w < units))
        def _():
            k, r = w // splits, lax.rem(w, splits)

            @pl.when(is_root & (r == 0))
            def _():
                def keep(q, _):
                    own[q, k] = full[lax.rem(home_s * c + q + 2 * col, n), k]
                    return 0

                lax.fori_loop(0, c, keep, 0)

            def some(i, _):
                multiply(k, r * share + i)
                return 0

            lax.fori_loop(0, share, some, 0)

        return 0

    lax.fori_loop(0, units + settle, step, 0)

    def finish(a, _):
        rows = pl.ds(pl.multiple_of(a * block, block), block)
        o_ref[rows, :] = o_ref[rows, :] * cond[rows, :]
        return 0

    lax.fori_loop(0, span * points // block, finish, 0)

    def drain(d, _):
        def piece_done(sems, j):
            pltpu.make_async_copy(full.at[0], full.at[0], sems.at[j]).wait()

        @pl.when(z >= d)
        def _():
            j = row - 2 * d

            @pl.when(z + 1 < m)
            def _():
                piece_done(up_send, j)

            piece_done(pair_send, j)

        @pl.when(z + d < m)
        def _():
            j = row + 2 * d

            @pl.when(z > 0)
            def _():
                piece_done(down_send, j)

            @pl.when(d > 0)
            def _():
                piece_done(pair_send, j)

        return 0

    lax.fori_loop(0, m, drain, 0)

    @pl.when(is_root)
    def _():
        for p in range(pairs):
            pltpu.make_async_copy(own, own, own_send.at[p]).wait()

    @pl.when(is_peer)
    def _():
        pltpu.make_async_copy(own, own, own_send.at[0]).wait()

    def drain_trade(k, _):
        @pl.when(keeps == 1)
        def _():
            rest = got.at[k, pl.ds(0, (n - 1) * cap)]
            pltpu.make_async_copy(rest, rest, trade_send.at[k]).wait()

        @pl.when(keeps == 0)
        def _():
            pltpu.make_async_copy(got.at[k], got.at[k], trade_send.at[k]).wait()

        return 0

    lax.fori_loop(0, chunks, drain_trade, 0)


def trade_spread_multiply(xv, xc, slots, n, c, cap):
    points = slots.shape[0]
    wv, wc = xv.shape[1], xc.shape[1]
    span = n // c
    pairs = c // 2
    g = math.gcd(wv, wc)
    chunks = (wv + wc) // g
    splits = max(points // UNIT_ROWS, 1)
    units = chunks * splits
    dma = pltpu.SemaphoreType.DMA
    return pl.pallas_call(
        functools.partial(gram_kernel, n, c, cap, wv // g, splits),
        out_shape=pltpu.VMEM((span * points, points), jnp.float32),
        in_specs=[
            pl.BlockSpec(memory_space=pl.ANY),
            pl.BlockSpec(memory_space=pl.ANY),
            pl.BlockSpec(memory_space=pltpu.VMEM),
        ],
        out_specs=pl.BlockSpec(memory_space=pltpu.VMEM),
        scratch_shapes=[
            pltpu.VMEM((chunks, n * cap, g), jnp.bfloat16),
            pltpu.VMEM((points, n * cap), jnp.bfloat16),
            pltpu.VMEM((n, chunks, points, g), jnp.bfloat16),
            pltpu.VMEM((c, chunks, points, g), jnp.bfloat16),
            pltpu.VMEM((span * points, points), jnp.float32),
            dma((chunks,)),
            dma((chunks,)),
            dma((n,)),
            dma((n,)),
            dma((n,)),
            dma((n, units)),
            dma((pairs,)),
            dma((c, units)),
        ],
        compiler_params=pltpu.CompilerParams(
            collective_id=0, has_side_effects=True, vmem_limit_bytes=50 * 1024 * 1024
        ),
    )(xv, xc, slots)


def on_device(valence, conduction, point_index):
    n = lax.axis_size("row")
    c = lax.axis_size("col")
    row, col = lax.axis_index("row"), lax.axis_index("col")
    grid_cells = valence.shape[0]
    points = point_index.shape[0] // n
    cap = max(2 * points // n, 2)
    blocks = point_index.reshape(n, points)
    owners = blocks // grid_cells
    offsets = blocks - owners * grid_cells
    onehot = owners[:, None, :] == jnp.arange(n, dtype=jnp.int32)[None, :, None]
    place = jnp.arange(points, dtype=jnp.int32)
    earlier = (place[:, None] < place[None, :]).astype(jnp.bfloat16)
    before = lax.dot_general(
        onehot.astype(jnp.bfloat16), earlier, (((2,), (0,)), ((), ())),
        preferred_element_type=jnp.float32,
    )
    ranks = jnp.sum(jnp.where(onehot, before, 0.0), axis=1).astype(jnp.int32)
    picked = (owners == row)[:, None, :] & (
        ranks[:, None, :] == jnp.arange(cap, dtype=jnp.int32)[None, :, None]
    )
    source_cells = jnp.sum(jnp.where(picked, offsets[:, None, :], 0), axis=2).reshape(n * cap)
    piece = lax.rem(row - 2 * col + 2 * n, n) // c + col * (n // c)
    slots = lax.dynamic_index_in_dim(owners * cap + ranks, piece, 0, keepdims=False)
    slots = jnp.broadcast_to(slots[:, None], (points, 128))
    xv = valence.at[source_cells].get(mode="promise_in_bounds")
    xc = conduction.at[source_cells].get(mode="promise_in_bounds")
    return trade_spread_multiply(xv, xc, slots, n, c, cap)


def solution(mesh):
    placed = (P("row", "col"), P("row", "col"), P())
    return jax.shard_map(
        on_device, mesh=mesh, in_specs=placed, out_specs=P("col", "row"), check_vma=False
    )
```

time: 290 us -> 263 us (0.907)
  waiting for transfers between devices: 56.5 us -> 0 us
  Pallas kernels: 180 us -> 232 us
  starting transfers between devices: 11.7 us -> 0 us
  local copies, waits for them, and re-layouts: 36.2 us -> 26.3 us
    all_to_all x2 -> x0, waiting for transfers between devices: 56.5 us -> none  [route(): got = lax.all_to_all(send, 'row', split_axis=0, concat_axis=0, tiled=True)]
    pallas_call x1, Pallas kernels: 180 us -> 232 us  [trade_spread_multiply(): pl.pallas_call(functools.partial(gram_kernel, n, c, cap, wv // g, splits)...]
    all_to_all x2 -> x0, starting transfers between devices: 11.7 us -> none  [route(): got = lax.all_to_all(send, 'row', split_axis=0, concat_axis=0, tiled=True)]
    gather x4 -> x2, local copies, waits for them, and re-layouts: 31.9 us -> 21 us  [the longest x1 12 us: on_device(): xv = valence.at[source_cells].get(mode='promise_in_bounds')]
  transfers between devices with their start and end apart: 2 -> 0, of which waited for: 2 -> 0; matrix products, arithmetic and copies ran while one was open for 6% -> 0% of each run, Pallas kernels for 0% -> 0%
where the time goes in v1:
time: 263 us; the launch traced here: 260 us
  Pallas kernels  232 us (88%)
  local copies, waits for them, and re-layouts  26.3 us (10%)
    pallas_call x1, Pallas kernels, trade_spread_multiply(): pl.pallas_call(functools.partial(gram_kernel, n, c, cap, wv // g, splits)...  232 us
    gather x1, local copies, waits for them, and re-layouts, on_device(): xv = valence.at[source_cells].get(mode='promise_in_bounds')  12 us
    gather x1, local copies, waits for them, and re-layouts, on_device(): xc = conduction.at[source_cells].get(mode='promise_in_bounds')  9 us

profile of v1, /device:TPU:0, one launch (start us, length us, event | category | flops | bytes accessed | tf_op | source)
XLA Modules:
  0.0 260.4 jit_solution(10762419174381007983)
XLA Ops:
  0.0 0.0 copy-start
  0.0 0.9 reshape.91
  1.0 0.4 fusion.7
  1.4 1.8 select_reduce_fusion
  3.3 1.0 broadcast_in_dim.38.slot_ref
  4.3 0.0 copy-done
  4.3 9.0 %gather_fusion.1 = bf16[2048,256]{1,0:T(8,128)(2,1)} fusion(bf16[4096,256]{1,0:T(8,128)(2,1)S(1)} %copy-done, s32[2048]{0:T(1024)S(1)} %broadcast_clamp_fusion), kind=kCustom, calls=%fused_computation.1 | custom fusion | bytes 2105344 | tf_op jit(solution)/shard_map/gather | solution.py:474
  13.3 12.0 %gather_fusion = bf16[2048,512]{1,0:T(8,128)(2,1)} fusion(bf16[4096,512]{1,0:T(8,128)(2,1)} %param.3, s32[2048]{0:T(1024)S(1)} %broadcast_clamp_fusion), kind=kCustom, calls=%fused_computation | custom fusion | bytes 4202496 | tf_op jit(solution)/shard_map/gather | solution.py:473
  25.3 231.6 %shard_map.37 = f32[2048,1024]{1,0:T(8,128)S(1)} custom-call(bf16[2048,512]{1,0:T(8,128)(2,1)} %gather_fusion, bf16[2048,256]{1,0:T(8,128)(2,1)} %gather_fusion.1, s32[1024,128]{1,0:T(8,128)} %broadcast_in_dim.38.slot_ref), custom_call_target="tpu_custom_call" | custom-call | tf_op jit(solution)/shard_map/pallas_call | solution.py:418
  257.0 3.4 %copy.6 = f32[2048,1024]{1,0:T(8,128)} copy(f32[2048,1024]{1,0:T(8,128)S(1)} %shard_map.37) | data formatting | bytes 16777216
  (7 shorter events, 0.1 us)
Async XLA Ops:
  0.0 4.3 %copy-start = (bf16[4096,256]{1,0:T(8,128)(2,1)S(1)}, bf16[4096,256]{1,0:T(8,128)(2,1)}, u32[]{:S(2)}) copy-start(bf16[4096,256]{1,0:T(8,128)(2,1)} %param.4) | copy-start | bytes 6291460

commit v2 on v1

v2 whole, which is shorter than its diff:
```python
import functools

import jax
import jax.numpy as jnp
from jax import lax
from jax.experimental import pallas as pl
from jax.experimental.pallas import tpu as pltpu
from jax.sharding import PartitionSpec as P

MESH = pl.DeviceIdType.MESH
UNIT_ROWS = 128
TILE = 256
LEAD = 1
HOP = 1
BAND = 1024


def gram_kernel(
    n, c, cap, kv, splits,
    val_ref, con_ref, cell_ref, slot_ref, o_ref,
    stage, wide, loose, packed, got, pick, full, own,
    load_sem, trade_send, trade_recv, up_send, down_send, pair_send, piece_recv, own_send, own_recv,
):
    chunks, _, g = got.shape
    points = slot_ref.shape[0]
    span = n // c
    pairs = c // 2
    m = n // 2
    block = 128
    rows_unit = points // splits
    units = chunks * splits
    share = n // splits
    row, col = lax.axis_index("row"), lax.axis_index("col")
    z, y = row // 2, lax.rem(row, 2)
    pair = row + 1 - 2 * y
    core, chip = lax.rem(col, 2), col // 2
    mate = chip * 2 + 1 - core
    home, home_s = row // span, lax.rem(row, span)
    home_core = lax.rem(home, 2)
    is_root = col == home
    is_peer = (core == home_core) & (col != home)
    is_far = core != home_core

    def part_of(p):
        t = lax.rem(p - 2 * col + 2 * n, n)
        return t // c, lax.rem(t, c)

    def place_of(s, q, k):
        return lax.rem(s * c + q + 2 * k, n)

    my_shard = part_of(row)[1]
    keeps = (my_shard == col).astype(jnp.int32)

    def trade_target(i):
        e = lax.rem(i + row, n)
        s, k = e // c, lax.rem(e, c)
        return place_of(s, col, k), k, s

    def load(k):
        src = val_ref if k < kv else con_ref
        first = (k if k < kv else k - kv) * g
        return pltpu.make_async_copy(src.at[:, pl.ds(first, g)], stage.at[k], load_sem.at[k])

    for k in range(chunks):
        load(k).start()

    barrier = pltpu.get_barrier_semaphore()

    def greet(r, k):
        pl.semaphore_signal(barrier, inc=1, device_id=(r, k), device_id_type=MESH)

    def greet_trade(i, _):
        target, k, _ = trade_target(i)

        @pl.when((target != row) | (k != col))
        def _():
            greet(target, k)

        @pl.when((i != row) | (my_shard != col))
        def _():
            greet(i, my_shard)

        return 0

    lax.fori_loop(0, n, greet_trade, 0)

    @pl.when(z > 0)
    def _():
        greet(row - 2, col)

    @pl.when(z + 1 < m)
    def _():
        greet(row + 2, col)

    greet(pair, col)
    greet(row, mate)
    for p in range(1, pairs):
        greet(row, lax.rem(chip + p, pairs) * 2 + core)
    ends = (z > 0).astype(jnp.int32) + (z + 1 < m).astype(jnp.int32)
    pl.semaphore_wait(barrier, 2 * (n - keeps) + ends + 2 + pairs - 1)

    messages = chunks * n
    cells = wide.shape[0]

    def message_rows(j):
        target, cd, s = trade_target(lax.rem(j, n))
        first = pl.multiple_of((cd * span + s) * cap, cap)
        return target, cd, j // n, first

    def widen(k):
        for a in range(chunks):
            @pl.when(k == a)
            def _():
                load(a).wait()

        def some(b, _):
            rows = pl.ds(pl.multiple_of(b * block, block), block)
            wide[rows, :] = stage[k, rows, :].astype(jnp.float32)
            return 0

        lax.fori_loop(0, cells // block, some, 0)

    def collect(j):
        _, _, k, first = message_rows(j)

        @pl.when(lax.rem(j, n) == 0)
        def _():
            widen(k)

        def some(a, _):
            base = pl.multiple_of(a * 16, 16)
            for r in range(16):
                cell = cell_ref[first + base + r]
                loose[pl.ds(base + r, 1), :] = wide[pl.ds(cell, 1), :]
            return 0

        lax.fori_loop(0, cap // 16, some, 0)
        packed[k, pl.ds(first, cap), :] = loose[...].astype(jnp.bfloat16)

    def ship(j):
        target, cd, k, first = message_rows(j)
        mine = pl.ds(pl.multiple_of(row * cap, cap), cap)
        stays = (target == row) & (cd == col)

        @pl.when(stays)
        def _():
            got[k, mine, :] = packed[k, pl.ds(first, cap), :]

        @pl.when(jnp.logical_not(stays))
        def _():
            pltpu.make_async_remote_copy(
                src_ref=packed.at[k, pl.ds(first, cap)], dst_ref=got.at[k, mine],
                send_sem=trade_send.at[k], recv_sem=trade_recv.at[k],
                device_id=(target, cd), device_id_type=MESH,
            ).start()

    def trade_portion(p):
        def one(i, _):
            j = p * share + i
            collect(j)

            @pl.when(j > 0)
            def _():
                ship(j - 1)

            return 0

        lax.fori_loop(0, share, one, 0)

    def opening(p, _):
        trade_portion(p)
        return 0

    lead = splits + min(LEAD, splits)
    lax.fori_loop(0, lead, opening, 0)

    lanes = 128

    def build_pick(a, _):
        first = pl.multiple_of(a * lanes, lanes)
        place = lax.broadcasted_iota(jnp.int32, (points, lanes), 1) + first
        chosen = slot_ref[...] == place
        pick[:, pl.ds(first, lanes)] = jnp.where(chosen, 1.0, 0.0).astype(jnp.bfloat16)
        return 0

    lax.fori_loop(0, n * cap // lanes, build_pick, 0)

    def unit_rows(u):
        return u // splits, pl.ds(pl.multiple_of(lax.rem(u, splits) * rows_unit, rows_unit), rows_unit)

    def unit(p, u):
        k, rows = unit_rows(u)
        return full.at[p, k, rows]

    def send(p, u, sems, target_row):
        ref = unit(p, u)
        return pltpu.make_async_remote_copy(
            src_ref=ref, dst_ref=ref,
            send_sem=sems.at[p], recv_sem=piece_recv.at[p, u],
            device_id=(target_row, col), device_id_type=MESH,
        )

    def own_copy(q, u, src, slot, target_col):
        k, rows = unit_rows(u)
        return pltpu.make_async_remote_copy(
            src_ref=src, dst_ref=own.at[q, k, rows],
            send_sem=own_send.at[slot], recv_sem=own_recv.at[q, u],
            device_id=(row, target_col), device_id_type=MESH,
        )

    def own_unit(q, u):
        k, rows = unit_rows(u)
        return own.at[q, k, rows]

    def route(p):
        oz, same = p // 2, lax.rem(p, 2) == y
        up = same & (z >= oz) & (z + 1 < m)
        down = same & (z <= oz) & (z > 0)
        hops = jnp.abs(z - oz) + jnp.where(same, 0, 1)
        return up, down, same, hops

    def spread(p, u):
        up, down, cross, _ = route(p)

        @pl.when(up)
        def _():
            send(p, u, up_send, row + 2).start()

        @pl.when(down)
        def _():
            send(p, u, down_send, row - 2).start()

        @pl.when(cross)
        def _():
            send(p, u, pair_send, pair).start()

        s, q = part_of(p)

        @pl.when(is_root & (s == home_s))
        def _():
            for a in range(1, pairs):
                own_copy(q, u, unit(p, u), a, lax.rem(chip + a, pairs) * 2 + core).start()
            own_copy(q, u, unit(p, u), 0, mate).start()

    def trade_done(sems, k):
        for kept in range(2):
            @pl.when(keeps == kept)
            def _():
                part = got.at[k, pl.ds(0, (n - kept) * cap)]
                pltpu.make_async_copy(part, part, sems.at[k]).wait()

    def compact(v):
        k, rows = unit_rows(v)

        @pl.when(lax.rem(v, splits) == 0)
        def _():
            trade_done(trade_recv, k)

        dense = lax.dot_general(
            pick[rows, :], got[k], (((1,), (0,)), ((), ())), preferred_element_type=jnp.float32
        )
        full[row, k, rows, :] = dense.astype(jnp.bfloat16)

    tile = min(TILE, points)
    band = min(BAND, points)
    items = span * (points // tile)

    def multiply(k, i):
        s, a = i // (points // tile), lax.rem(i, points // tile)
        cols = pl.ds(pl.multiple_of(a * tile, tile), tile)

        def strip(b, _):
            inner = pl.ds(pl.multiple_of(b * band, band), band)
            rows = pl.ds(pl.multiple_of(s * points + b * band, band), band)
            total = None
            for q in range(c):
                part = lax.dot_general(
                    full[place_of(s, q, col), k, inner, :], own[q, k, cols, :],
                    (((1,), (1,)), ((), ())), preferred_element_type=jnp.float32,
                )
                total = part if total is None else total + part

            @pl.when(k == 0)
            def _():
                o_ref[rows, cols] = total

            @pl.when((k > 0) & (k < kv))
            def _():
                o_ref[rows, cols] += total

            @pl.when(k == kv)
            def _():
                o_ref[rows, cols] *= total

            return 0

        lax.fori_loop(0, points // band, strip, 0)

    compact(0)
    settle = HOP * (m + 2) + splits - 1

    def step(t, _):
        @pl.when(t + lead < units)
        def _():
            trade_portion(t + lead)

        @pl.when(t + lead == units)
        def _():
            ship(messages - 1)

        @pl.when(t < units)
        def _():
            spread(row, t)

        def pieces(p, _):
            hops = route(p)[3]
            u = t - HOP * hops

            @pl.when((hops > 0) & (u >= 0) & (u < units))
            def _():
                send(p, u, pair_send, pair).wait_recv()
                spread(p, u)

            return 0

        @pl.when(t + 1 < units)
        def _():
            compact(t + 1)

        lax.fori_loop(0, n, pieces, 0)

        def take_peer(q, _):
            u = t - HOP * (m + 1)

            @pl.when(is_peer & (u >= 0) & (u < units))
            def _():
                copy = own_copy(q, u, own_unit(q, u), 0, mate)
                copy.wait_recv()
                copy.start()

            return 0

        lax.fori_loop(0, c, take_peer, 0)

        def take_far(q, _):
            u = t - HOP * (m + 2)

            @pl.when(is_far & (u >= 0) & (u < units))
            def _():
                own_copy(q, u, own_unit(q, u), 0, mate).wait_recv()

            return 0

        lax.fori_loop(0, c, take_far, 0)

        w = t - settle

        @pl.when((w >= 0) & (w < units))
        def _():
            k, r = w // splits, lax.rem(w, splits)

            @pl.when(is_root & (r == 0))
            def _():
                def keep(q, _):
                    own[q, k] = full[place_of(home_s, q, col), k]
                    return 0

                lax.fori_loop(0, c, keep, 0)

            def some(i, _):
                multiply(k, r * (items // splits) + i)
                return 0

            lax.fori_loop(0, items // splits, some, 0)

        return 0

    lax.fori_loop(0, units + settle, step, 0)

    def drain(p, _):
        up, down, cross, _ = route(p)

        def piece_done(sems):
            pltpu.make_async_copy(full.at[0], full.at[0], sems.at[p]).wait()

        for goes, sems in ((up, up_send), (down, down_send), (cross, pair_send)):
            @pl.when(goes)
            def _():
                piece_done(sems)

        return 0

    lax.fori_loop(0, n, drain, 0)

    @pl.when(is_root)
    def _():
        for p in range(pairs):
            pltpu.make_async_copy(own, own, own_send.at[p]).wait()

    @pl.when(is_peer)
    def _():
        pltpu.make_async_copy(own, own, own_send.at[0]).wait()

    def drain_trade(k, _):
        trade_done(trade_send, k)
        return 0

    lax.fori_loop(0, chunks, drain_trade, 0)


def trade_spread_multiply(valence, conduction, source, slots, n, c, cap):
    points = slots.shape[0]
    wv, wc = valence.shape[1], conduction.shape[1]
    cells = valence.shape[0]
    span = n // c
    pairs = c // 2
    g = wc
    chunks = (wv + wc) // g
    splits = max(points // UNIT_ROWS, 1)
    units = chunks * splits
    dma = pltpu.SemaphoreType.DMA
    return pl.pallas_call(
        functools.partial(gram_kernel, n, c, cap, wv // g, splits),
        out_shape=pltpu.VMEM((span * points, points), jnp.float32),
        in_specs=[
            pl.BlockSpec(memory_space=pl.ANY),
            pl.BlockSpec(memory_space=pl.ANY),
            pl.BlockSpec(memory_space=pltpu.SMEM),
            pl.BlockSpec(memory_space=pltpu.VMEM),
        ],
        out_specs=pl.BlockSpec(memory_space=pltpu.VMEM),
        scratch_shapes=[
            pltpu.VMEM((chunks, cells, g), jnp.bfloat16),
            pltpu.VMEM((cells, g), jnp.float32),
            pltpu.VMEM((cap, g), jnp.float32),
            pltpu.VMEM((chunks, n * cap, g), jnp.bfloat16),
            pltpu.VMEM((chunks, n * cap, g), jnp.bfloat16),
            pltpu.VMEM((points, n * cap), jnp.bfloat16),
            pltpu.VMEM((n, chunks, points, g), jnp.bfloat16),
            pltpu.VMEM((c, chunks, points, g), jnp.bfloat16),
            dma((chunks,)),
            dma((chunks,)),
            dma((chunks,)),
            dma((n,)),
            dma((n,)),
            dma((n,)),
            dma((n, units)),
            dma((pairs,)),
            dma((c, units)),
        ],
        compiler_params=pltpu.CompilerParams(
            collective_id=0, has_side_effects=True, vmem_limit_bytes=50 * 1024 * 1024
        ),
    )(valence, conduction, source, slots)


def on_device(valence, conduction, point_index):
    n = lax.axis_size("row")
    c = lax.axis_size("col")
    row, col = lax.axis_index("row"), lax.axis_index("col")
    grid_cells = valence.shape[0]
    points = point_index.shape[0] // n
    cap = max(2 * points // n, 2)
    blocks = point_index.reshape(n, points)
    owners = blocks // grid_cells
    offsets = blocks - owners * grid_cells
    onehot = owners[:, None, :] == jnp.arange(n, dtype=jnp.int32)[None, :, None]
    place = jnp.arange(points, dtype=jnp.int32)
    earlier = (place[:, None] < place[None, :]).astype(jnp.bfloat16)
    before = lax.dot_general(
        onehot.astype(jnp.bfloat16), earlier, (((2,), (0,)), ((), ())),
        preferred_element_type=jnp.float32,
    )
    ranks = jnp.sum(jnp.where(onehot, before, 0.0), axis=1).astype(jnp.int32)
    picked = (owners == row)[:, None, :] & (
        ranks[:, None, :] == jnp.arange(cap, dtype=jnp.int32)[None, :, None]
    )
    source_cells = jnp.sum(jnp.where(picked, offsets[:, None, :], 0), axis=2).reshape(n * cap)
    piece = lax.rem(row - 2 * col + 2 * n, n) // c + col * (n // c)
    slots = lax.dynamic_index_in_dim(owners * cap + ranks, piece, 0, keepdims=False)
    slots = jnp.broadcast_to(slots[:, None], (points, 128))
    return trade_spread_multiply(valence, conduction, source_cells, slots, n, c, cap)


def solution(mesh):
    placed = (P("row", "col"), P("row", "col"), P())
    return jax.shard_map(
        on_device, mesh=mesh, in_specs=placed, out_specs=P("col", "row"), check_vma=False
    )
```

time: 263 us -> 230 us (0.87)
  local copies, waits for them, and re-layouts: 26.3 us -> 5.76 us
  Pallas kernels: 232 us -> 221 us
    gather x2 -> x0, local copies, waits for them, and re-layouts: 21 us -> none  [the longest x1 12 us: on_device(): xv = valence.at[source_cells].get(mode='promise_in_bounds')]
    pallas_call x1, Pallas kernels: 232 us -> 221 us  [trade_spread_multiply(): pl.pallas_call(functools.partial(gram_kernel, n, c, cap, wv // g, splits)...]
where the time goes in v2:
time: 230 us; the launch traced here: 229 us
  Pallas kernels  221 us (96%)
  local copies, waits for them, and re-layouts  5.76 us (3%)
    pallas_call x1, Pallas kernels, trade_spread_multiply(): pl.pallas_call(functools.partial(gram_kernel, n, c, cap, wv // g, splits)...  221 us

profile of v2, /device:TPU:0, one launch (start us, length us, event | category | flops | bytes accessed | tf_op | source)
XLA Modules:
  0.0 229.4 jit_solution(9529167648602272468)
XLA Ops:
  0.0 0.8 reshape.63
  0.8 0.4 fusion.7
  1.3 1.8 select_reduce_fusion
  3.1 0.6 copy.4
  3.7 1.0 broadcast_in_dim.36.slot_ref
  4.7 221.3 %shard_map.37 = f32[2048,1024]{1,0:T(8,128)S(1)} custom-call(bf16[4096,512]{1,0:T(8,128)(2,1)} %val_ref.1, bf16[4096,256]{1,0:T(8,128)(2,1)} %con_ref.1, s32[2048]{0:T(1024)} %bitcast.10, s32[1024,128]{1,0:T(8,128)} %broadcast_in_dim.36.slot_ref), custom_call_target="tpu_custom_call" | custom-call | tf_op jit(solution)/shard_map/pallas_call | solution.py:422
  226.0 3.4 %copy.6 = f32[2048,1024]{1,0:T(8,128)} copy(f32[2048,1024]{1,0:T(8,128)S(1)} %shard_map.37) | data formatting | bytes 16777216
  (4 shorter events, 0.1 us)

commit v3 on v2

--- a/solution.py
+++ b/solution.py
@@ -8,17 +8,18 @@
 from jax.sharding import PartitionSpec as P
 
 MESH = pl.DeviceIdType.MESH
-UNIT_ROWS = 128
+UNIT_ROWS = 256
+LANES = 128
+FLAT = 4
 TILE = 256
 LEAD = 1
 HOP = 1
-BAND = 1024
 
 
 def gram_kernel(
-    n, c, cap, kv, splits,
+    n, c, cap, kv, splits, fold,
     val_ref, con_ref, cell_ref, slot_ref, o_ref,
-    stage, wide, loose, packed, got, pick, full, own,
+    stage, wide, loose, packed, got, pick, full, own, cond,
     load_sem, trade_send, trade_recv, up_send, down_send, pair_send, piece_recv, own_send, own_recv,
 ):
     chunks, _, g = got.shape
@@ -57,11 +58,11 @@
         return place_of(s, col, k), k, s
 
     def load(k):
-        src = val_ref if k < kv else con_ref
-        first = (k if k < kv else k - kv) * g
-        return pltpu.make_async_copy(src.at[:, pl.ds(first, g)], stage.at[k], load_sem.at[k])
-
-    for k in range(chunks):
+        src = val_ref if k * fold < kv else con_ref
+        first = (k * fold if k * fold < kv else k * fold - kv) * g
+        return pltpu.make_async_copy(src.at[:, pl.ds(first, fold * g)], stage.at[k], load_sem.at[k])
+
+    for k in range(chunks // fold):
         load(k).start()
 
     barrier = pltpu.get_barrier_semaphore()
@@ -108,7 +109,7 @@
         return target, cd, j // n, first
 
     def widen(k):
-        for a in range(chunks):
+        for a in range(chunks // fold):
             @pl.when(k == a)
             def _():
                 load(a).wait()
@@ -123,19 +124,22 @@
     def collect(j):
         _, _, k, first = message_rows(j)
 
-        @pl.when(lax.rem(j, n) == 0)
-        def _():
-            widen(k)
-
-        def some(a, _):
-            base = pl.multiple_of(a * 16, 16)
-            for r in range(16):
-                cell = cell_ref[first + base + r]
-                loose[pl.ds(base + r, 1), :] = wide[pl.ds(cell, 1), :]
-            return 0
-
-        lax.fori_loop(0, cap // 16, some, 0)
-        packed[k, pl.ds(first, cap), :] = loose[...].astype(jnp.bfloat16)
+        @pl.when(lax.rem(j, n * fold) == 0)
+        def _():
+            widen(k // fold)
+
+        @pl.when(lax.rem(k, fold) == 0)
+        def _():
+            def some(a, _):
+                base = pl.multiple_of(a * 16, 16)
+                for r in range(16):
+                    cell = cell_ref[first + base + r]
+                    loose[pl.ds(base + r, 1), :] = wide[pl.ds(cell, 1), :]
+                return 0
+
+            lax.fori_loop(0, cap // 16, some, 0)
+            for f in range(fold):
+                packed[k + f, pl.ds(first, cap), :] = loose[:, f * g : (f + 1) * g].astype(jnp.bfloat16)
 
     def ship(j):
         target, cd, k, first = message_rows(j)
@@ -212,25 +216,27 @@
         k, rows = unit_rows(u)
         return own.at[q, k, rows]
 
-    def route(p):
+    def place(p):
         oz, same = p // 2, lax.rem(p, 2) == y
-        up = same & (z >= oz) & (z + 1 < m)
-        down = same & (z <= oz) & (z > 0)
+        rim = (oz == 0) | (oz == m - 1)
+        rises = (z >= oz) & (z + 1 < m)
+        falls = (z <= oz) & (z > 0)
         hops = jnp.abs(z - oz) + jnp.where(same, 0, 1)
-        return up, down, same, hops
+        return same, rim, rises, falls, z == oz, hops
 
     def spread(p, u):
-        up, down, cross, _ = route(p)
-
-        @pl.when(up)
+        same, rim, rises, falls, level, _ = place(p)
+        flat = rim & (lax.rem(u, FLAT) == 0)
+
+        @pl.when((same | flat) & rises)
         def _():
             send(p, u, up_send, row + 2).start()
 
-        @pl.when(down)
+        @pl.when((same | flat) & falls)
         def _():
             send(p, u, down_send, row - 2).start()
 
-        @pl.when(cross)
+        @pl.when(same & (level | jnp.logical_not(flat)))
         def _():
             send(p, u, pair_send, pair).start()
 
@@ -262,39 +268,41 @@
         full[row, k, rows, :] = dense.astype(jnp.bfloat16)
 
     tile = min(TILE, points)
-    band = min(BAND, points)
     items = span * (points // tile)
 
     def multiply(k, i):
         s, a = i // (points // tile), lax.rem(i, points // tile)
         cols = pl.ds(pl.multiple_of(a * tile, tile), tile)
-
-        def strip(b, _):
-            inner = pl.ds(pl.multiple_of(b * band, band), band)
-            rows = pl.ds(pl.multiple_of(s * points + b * band, band), band)
-            total = None
-            for q in range(c):
-                part = lax.dot_general(
-                    full[place_of(s, q, col), k, inner, :], own[q, k, cols, :],
-                    (((1,), (1,)), ((), ())), preferred_element_type=jnp.float32,
-                )
-                total = part if total is None else total + part
-
-            @pl.when(k == 0)
-            def _():
-                o_ref[rows, cols] = total
-
-            @pl.when((k > 0) & (k < kv))
-            def _():
-                o_ref[rows, cols] += total
-
-            @pl.when(k == kv)
-            def _():
-                o_ref[rows, cols] *= total
-
-            return 0
-
-        lax.fori_loop(0, points // band, strip, 0)
+        rows = pl.ds(pl.multiple_of(s * points, points), points)
+        total = None
+        for q in range(0, c, 2):
+            left = jnp.concatenate([full[place_of(s, q + e, col), k] for e in range(2)], axis=1)
+            right = jnp.concatenate([own[q + e, k, cols, :] for e in range(2)], axis=1)
+            part = lax.dot_general(
+                left, right, (((1,), (1,)), ((), ())), preferred_element_type=jnp.float32
+            )
+            total = part if total is None else total + part
+
+        @pl.when(k == 0)
+        def _():
+            o_ref[rows, cols] = total
+
+        @pl.when((k > 0) & (k < kv))
+        def _():
+            o_ref[rows, cols] += total
+
+        @pl.when((k == kv) & (k < chunks - 1))
+        def _():
+            cond[rows, cols] = total
+
+        @pl.when((k > kv) & (k < chunks - 1))
+        def _():
+            cond[rows, cols] += total
+
+        @pl.when(k == chunks - 1)
+        def _():
+            whole = total if chunks - kv == 1 else cond[rows, cols] + total
+            o_ref[rows, cols] *= whole
 
     compact(0)
     settle = HOP * (m + 2) + splits - 1
@@ -313,7 +321,7 @@
             spread(row, t)
 
         def pieces(p, _):
-            hops = route(p)[3]
+            hops = place(p)[5]
             u = t - HOP * hops
 
             @pl.when((hops > 0) & (u >= 0) & (u < units))
@@ -377,16 +385,27 @@
 
     lax.fori_loop(0, units + settle, step, 0)
 
+    flats = (units + FLAT - 1) // FLAT
+
+    def sent(sems, p, count):
+        part = stage.at[0, pl.ds(0, count * rows_unit // fold)]
+        pltpu.make_async_copy(part, part, sems.at[p]).wait()
+
     def drain(p, _):
-        up, down, cross, _ = route(p)
-
-        def piece_done(sems):
-            pltpu.make_async_copy(full.at[0], full.at[0], sems.at[p]).wait()
-
-        for goes, sems in ((up, up_send), (down, down_send), (cross, pair_send)):
+        same, rim, rises, falls, level, _ = place(p)
+        other = jnp.logical_not(same)
+        short = rim & jnp.logical_not(level)
+        for goes, sems, count in (
+            (same & rises, up_send, units),
+            (same & falls, down_send, units),
+            (other & rim & rises, up_send, flats),
+            (other & rim & falls, down_send, flats),
+            (same & jnp.logical_not(short), pair_send, units),
+            (same & short, pair_send, units - flats),
+        ):
             @pl.when(goes)
             def _():
-                piece_done(sems)
+                sent(sems, p, count)
 
         return 0
 
@@ -414,13 +433,14 @@
     cells = valence.shape[0]
     span = n // c
     pairs = c // 2
-    g = wc
+    g = LANES
+    fold = 2 if wv % (2 * g) == 0 and wc % (2 * g) == 0 else 1
     chunks = (wv + wc) // g
     splits = max(points // UNIT_ROWS, 1)
     units = chunks * splits
     dma = pltpu.SemaphoreType.DMA
     return pl.pallas_call(
-        functools.partial(gram_kernel, n, c, cap, wv // g, splits),
+        functools.partial(gram_kernel, n, c, cap, wv // g, splits, fold),
         out_shape=pltpu.VMEM((span * points, points), jnp.float32),
         in_specs=[
             pl.BlockSpec(memory_space=pl.ANY),
@@ -430,15 +450,16 @@
         ],
         out_specs=pl.BlockSpec(memory_space=pltpu.VMEM),
         scratch_shapes=[
-            pltpu.VMEM((chunks, cells, g), jnp.bfloat16),
-            pltpu.VMEM((cells, g), jnp.float32),
-            pltpu.VMEM((cap, g), jnp.float32),
+            pltpu.VMEM((chunks // fold, cells, fold * g), jnp.bfloat16),
+            pltpu.VMEM((cells, fold * g), jnp.float32),
+            pltpu.VMEM((cap, fold * g), jnp.float32),
             pltpu.VMEM((chunks, n * cap, g), jnp.bfloat16),
             pltpu.VMEM((chunks, n * cap, g), jnp.bfloat16),
             pltpu.VMEM((points, n * cap), jnp.bfloat16),
             pltpu.VMEM((n, chunks, points, g), jnp.bfloat16),
             pltpu.VMEM((c, chunks, points, g), jnp.bfloat16),
-            dma((chunks,)),
+            pltpu.VMEM((span * points, points), jnp.float32),
+            dma((chunks // fold,)),
             dma((chunks,)),
             dma((chunks,)),
             dma((n,)),

time: 230 us -> 213 us (0.926)
  Pallas kernels: 221 us -> 205 us
    pallas_call x1, Pallas kernels: 221 us -> 205 us  [trade_spread_multiply(): pl.pallas_call(functools.partial(gram_kernel, n, c, cap, wv // g, splits,...]
where the time goes in v3:
time: 213 us
  Pallas kernels  205 us (96%)
  local copies, waits for them, and re-layouts  5.76 us (3%)
    pallas_call x1, Pallas kernels, trade_spread_multiply(): pl.pallas_call(functools.partial(gram_kernel, n, c, cap, wv // g, splits,...  205 us

profile of v3, /device:TPU:0, one launch (start us, length us, event | category | flops | bytes accessed | tf_op | source)
XLA Modules:
  0.0 212.8 jit_solution(14707119174388432796)
XLA Ops:
  0.0 0.8 reshape.63
  0.8 0.4 fusion.7
  1.3 1.8 select_reduce_fusion
  3.1 0.6 copy.4
  3.7 1.0 broadcast_in_dim.36.slot_ref
  4.7 204.6 %shard_map.37 = f32[2048,1024]{1,0:T(8,128)S(1)} custom-call(bf16[4096,512]{1,0:T(8,128)(2,1)} %val_ref.1, bf16[4096,256]{1,0:T(8,128)(2,1)} %con_ref.1, s32[2048]{0:T(1024)} %bitcast.10, s32[1024,128]{1,0:T(8,128)} %broadcast_in_dim.36.slot_ref), custom_call_target="tpu_custom_call" | custom-call | tf_op jit(solution)/shard_map/pallas_call | solution.py:442
  209.4 3.4 %copy.6 = f32[2048,1024]{1,0:T(8,128)} copy(f32[2048,1024]{1,0:T(8,128)S(1)} %shard_map.37) | data formatting | bytes 16777216
  (4 shorter events, 0.1 us)

commit v4 on v3

--- a/solution.py
+++ b/solution.py
@@ -12,7 +12,7 @@
 LANES = 128
 FLAT = 4
 TILE = 256
-LEAD = 1
+LEAD = 2
 HOP = 1
 
 
@@ -256,16 +256,15 @@
                 pltpu.make_async_copy(part, part, sems.at[k]).wait()
 
     def compact(v):
-        k, rows = unit_rows(v)
+        k = v // splits
 
         @pl.when(lax.rem(v, splits) == 0)
         def _():
             trade_done(trade_recv, k)
-
-        dense = lax.dot_general(
-            pick[rows, :], got[k], (((1,), (0,)), ((), ())), preferred_element_type=jnp.float32
-        )
-        full[row, k, rows, :] = dense.astype(jnp.bfloat16)
+            dense = lax.dot_general(
+                pick[...], got[k], (((1,), (0,)), ((), ())), preferred_element_type=jnp.float32
+            )
+            full[row, k] = dense.astype(jnp.bfloat16)
 
     tile = min(TILE, points)
     items = span * (points // tile)

time: 213 us -> 210 us (0.986)
  Pallas kernels: 205 us -> 201 us
    pallas_call x1, Pallas kernels: 205 us -> 201 us  [trade_spread_multiply(): pl.pallas_call(functools.partial(gram_kernel, n, c, cap, wv // g, splits,...]
where the time goes in v4:
time: 210 us
  Pallas kernels  201 us (96%)
  local copies, waits for them, and re-layouts  5.76 us (3%)
    pallas_call x1, Pallas kernels, trade_spread_multiply(): pl.pallas_call(functools.partial(gram_kernel, n, c, cap, wv // g, splits,...  201 us

profile of v4, /device:TPU:0, one launch (start us, length us, event | category | flops | bytes accessed | tf_op | source)
XLA Modules:
  0.0 209.6 jit_solution(2924717323040254694)
XLA Ops:
  0.0 0.8 reshape.63
  0.8 0.4 fusion.7
  1.3 1.8 select_reduce_fusion
  3.1 0.6 copy.4
  3.7 1.0 broadcast_in_dim.36.slot_ref
  4.7 201.4 %shard_map.37 = f32[2048,1024]{1,0:T(8,128)S(1)} custom-call(bf16[4096,512]{1,0:T(8,128)(2,1)} %val_ref.1, bf16[4096,256]{1,0:T(8,128)(2,1)} %con_ref.1, s32[2048]{0:T(1024)} %bitcast.10, s32[1024,128]{1,0:T(8,128)} %broadcast_in_dim.36.slot_ref), custom_call_target="tpu_custom_call" | custom-call | tf_op jit(solution)/shard_map/pallas_call | solution.py:441
  206.2 3.4 %copy.6 = f32[2048,1024]{1,0:T(8,128)} copy(f32[2048,1024]{1,0:T(8,128)S(1)} %shard_map.37) | data formatting | bytes 16777216
  (4 shorter events, 0.1 us)
